TPU v7x, 32 devices: a whole 2x2x4 slice. The times are simulated.
32 devices in a mesh: groups: 2 (over x), rows: 16 (over z, y, core).
Axes of the slice: x: 2, y: 2, z: 4, core: 2. Of those that a mesh axis runs over, the one named last changes fastest.
Arguments:
- frames: bfloat16 [16384, 2560], P(('groups', 'rows')), parts along dimension 0, may hold values from -6 to 6
- offsets: int32 [4096], P(('groups', 'rows')), parts along dimension 0, may hold values from 0 to 8173, as said below
- neighbours: int32 [32, 4096], P(None, ('groups', 'rows')), parts along dimension 1, may hold values from 0 to 2047, as said below
- initial_codes: int32 [32, 4096], P(None, ('groups', 'rows')), parts along dimension 1, may hold values from -1048576 to 1048575
- embed_weight: bfloat16 [2560, 256], replicated, may hold values from -0.125 to 0.125
- embed_bias: float32 [256], replicated, may hold values from -0.9 to 0.9
Outputs:
- affinity: float32 [32, 4096], P(None, ('groups', 'rows')), parts along dimension 1
- vectors: float32 [32, 4096], P(None, ('groups', 'rows')), parts along dimension 1
There are 2 independent parts, one for each index of `groups`. A program takes and returns all parts, laid end to end along the dimension named above; an argument that names none is the same for every part. Nothing has to cross between parts.
Inputs may be any that keep to these rules, and one draw needn't show every extreme that they name: `offsets`: the window of row i starts in the block of 512 frames numbered i // 128 and its 19 frames end before frame 8192. `neighbours`: the 32 columns of row i are distinct and differ from i; the k-th is (i + d) mod 2048 with 1 + k s <= d <= (k + 1) s, where s = 63.
All inputs are finite; a program needn't handle non-finite values.
Results may differ from a plain program's by a relative error of at most 0.012.
The roundings to bfloat16 on the way count: a program that leaves them out, or rounds other values in their place, can miss the bound.
Values may be sent and summed in bfloat16 or wider, within the bound.
No kernel may reach another device: no remote copies, remote signals or barrier semaphores. Data moves between devices by JAX's collectives and lax.ppermute only.
A program may use at most 64 MiB of HBM per device.

v0:
```python
import jax
import jax.numpy as jnp
from jax import lax
from jax.sharding import PartitionSpec as P

WIN = 19
ITERS = 3
epsilon = 1e-06
sharpness = 8.0
seed_scale = 2.0 ** (-20)


def from_behind(block, axis, distance):
    devices = range(lax.axis_size(axis))
    route = [(i - distance, i) for i in devices if i - distance in devices]
    return lax.ppermute(block, axis, route)


def block_width(length, shard_rows):
    shards = length // shard_rows
    chosen = 1
    for factor in range(1, shards + 1):
        if shards % factor == 0 and factor * shard_rows <= 4096:
            chosen = factor
    return chosen * shard_rows


def on_device(frames, offsets, neighbours, initial_codes, embed_weight, embed_bias):
    own_rows = offsets.shape[0]
    own_frames = frames.shape[0]
    kept = neighbours.shape[0]
    my_index = lax.axis_index("rows")
    next_frames = from_behind(frames[: WIN - 1], "rows", -1)
    extended = jnp.concatenate([frames, next_frames], axis=0)
    window_start = offsets - my_index * own_frames
    positions = jnp.arange(extended.shape[0], dtype=jnp.int32)[None, :]
    begins = window_start[:, None]
    window_mask = ((positions >= begins) & (positions < begins + WIN)).astype(jnp.bfloat16)
    window_sums = jnp.dot(window_mask, extended, preferred_element_type=jnp.float32)
    pooled = (window_sums * (1.0 / WIN)).astype(jnp.bfloat16)
    embedded = jnp.dot(pooled, embed_weight, preferred_element_type=jnp.float32) + embed_bias
    squares = jnp.sum(embedded * embedded, axis=1, keepdims=True)
    unit_rows = (embedded * lax.rsqrt(squares + epsilon)).astype(jnp.bfloat16)
    portion = lax.all_gather(unit_rows, "rows", axis=0, tiled=True)
    length = portion.shape[0]
    block_cols = block_width(length, own_rows)

    def one_block(block_index, carried):
        first_col = block_index * block_cols
        candidates = lax.dynamic_slice_in_dim(portion, first_col, block_cols, 0)
        scores = lax.dot_general(
            unit_rows, candidates, (((1,), (1,)), ((), ())), preferred_element_type=jnp.float32
        )
        relative = neighbours - first_col
        inside = (relative >= 0) & (relative < block_cols)
        picked = jnp.take_along_axis(scores, jnp.clip(relative, 0, block_cols - 1).T, axis=1).T
        return carried + jnp.where(inside, picked, 0.0)

    cosine = lax.fori_loop(
        0, length // block_cols, one_block, jnp.zeros((kept, own_rows), jnp.float32)
    )
    affinity = jnp.exp(sharpness * (cosine - 1.0))
    vectors = initial_codes.astype(jnp.float32) * seed_scale
    vec_count = vectors.shape[0]
    carried = vectors
    for turn_index in range(ITERS):
        gathered = lax.all_gather(carried, "rows", axis=1, tiled=True)
        if turn_index > 0:
            gram_matrix = jnp.dot(gathered, gathered.T, precision=lax.Precision.HIGHEST)
            cholesky_factor = jnp.linalg.cholesky(gram_matrix)
            gathered = jax.scipy.linalg.solve_triangular(cholesky_factor, gathered, lower=True)
        current = lax.dynamic_slice_in_dim(gathered, my_index * own_rows, own_rows, 1)
        forward = jnp.sum(affinity[None] * jnp.take(gathered, neighbours, axis=1), axis=1)
        spread = (
            jnp.zeros((vec_count, gathered.shape[1]), jnp.float32)
            .at[:, neighbours.reshape(-1)]
            .add((affinity[None] * current[:, None, :]).reshape(vec_count, -1))
        )
        mixed = 0.5 * (forward + lax.psum_scatter(spread, "rows", scatter_dimension=1, tiled=True))
        carried = mixed
    partial_gram = jnp.dot(carried, carried.T, precision=lax.Precision.HIGHEST)
    gram_matrix = lax.psum(partial_gram, "rows")
    cholesky_factor = jnp.linalg.cholesky(gram_matrix)
    carried = jax.scipy.linalg.solve_triangular(cholesky_factor, carried, lower=True)
    return (affinity, carried)


def solution(mesh):
    placed = (
        P(("groups", "rows"), None),
        P(("groups", "rows")),
        P(None, ("groups", "rows")),
        P(None, ("groups", "rows")),
        P(),
        P(),
    )
    return jax.shard_map(
        on_device,
        mesh=mesh,
        in_specs=placed,
        out_specs=(P(None, ("groups", "rows")), P(None, ("groups", "rows"))),
        check_vma=False,
    )
```

profile of v0, /device:TPU:0, one launch (start us, length us, event | category | flops | bytes accessed | tf_op | source)
XLA Modules:
  0.0 474.0 jit_solution(6266484893465082726)
XLA Ops:
  7.2 1.0 slice.17
  8.2 1.3 collective-permute-start
  9.5 0.7 broadcast_add_fusion
  10.2 1.3 collective-permute-done
  11.5 2.9 multiply_reduce_fusion
  14.3 0.7 multiply_convert_fusion
  15.4 25.2 %all_gather.13 = f32[32,2048]{1,0:T(8,128)S(1)} all-gather(f32[32,128]{1,0:T(8,128)S(1)} %convert_multiply_fusion), channel_id=1, replica_groups=mesh['groups'=2,'rows'=16] {'rows'}, dimensions={1}, use_global_device_ids=true | all-gather | bytes 278528 | tf_op jit(solution)/shard_map/all_gather | solution.py:67
  41.1 14.1 %gather_fusion.1 = f32[4096,32]{1,0:T(8,128)} fusion(f32[32,2048]{0,1:T(8,128)S(1)} %copy.50, s32[4096]{0:T(1024)S(1)} %bitcast_clamp_fusion), kind=kCustom, calls=%fused_computation.clone | custom fusion | bytes 1064960 | tf_op jit(solution)/shard_map/jit(_take)/gather | solution.py:73
  55.2 3.1 all-gather.2.cloned.1.call-done
  58.3 1.7 fusion.64
  60.0 32.8 %gather_fusion = f32[4096]{0:T(1024)S(1)} fusion(f32[128,2048]{1,0:T(8,128)S(1)} %fusion.64, s32[4096]{0:T(1024)S(1)} %reshape.113), kind=kCustom, calls=%fused_computation.3 | custom fusion | bytes 65536 | tf_op jit(solution)/shard_map/while/body/eval_jaxpr/jit(take_along_axis)/gather | solution.py:56
  93.6 23.4 %scatter_custom_fusion = f32[32,2048]{0,1:T(8,128)} fusion(s32[4096]{0:T(1024)S(1)} %bitcast.98, f32[32,4096]{0,1:T(8,128)S(1)} %bitcast_multiply_fusion.4, f32[]{:T(128)} %constant.102.clone.1), kind=kCustom, calls=%fused_computation.22 | custom fusion | flops 131072 | bytes 2359300 | tf_op jit(solution)/shard_map/scatter-add | solution.py:77
  117.1 3.2 fusion.12
  120.3 53.4 %reduce-scatter.4.cloned.1.call-done = f32[32,128]{0,1:T(8,128)} async-done(((f32[32,2048]{0,1:T(8,128)}), f32[32,128]{0,1:T(8,128)}) %reduce-scatter.4.cloned.1.call-update) | async-done | bytes 16400 | tf_op jit(solution)/shard_map/reduce_scatter | solution.py:79
  173.7 0.8 add_multiply_fusion.2
  174.6 22.6 %all_gather.14 = f32[32,2048]{0,1:T(8,128)S(1)} all-gather(f32[32,128]{0,1:T(8,128)S(1)} %add_multiply_fusion.2), channel_id=1, replica_groups=mesh['groups'=2,'rows'=16] {'rows'}, dimensions={1}, use_global_device_ids=true | all-gather | bytes 278528 | tf_op jit(solution)/shard_map/all_gather | solution.py:67
  197.1 1.8 fusion.65
  199.0 2.9 cholesky.59
  202.0 0.6 compare_reduce_fusion.2
  202.6 0.7 fusion.40
  203.3 2.4 custom-call.13
  205.7 1.2 fusion.48
  207.0 0.7 copy-done.2
  208.4 23.4 %scatter_custom_fusion.1 = f32[32,2048]{0,1:T(8,128)} fusion(s32[4096]{0:T(1024)S(1)} %bitcast.99, f32[32,4096]{0,1:T(8,128)S(1)} %bitcast_multiply_fusion.2, f32[]{:T(128)} %constant.102.clone.1), kind=kCustom, calls=%fused_computation.17 | custom fusion | flops 131072 | bytes 2359300 | tf_op jit(solution)/shard_map/scatter-add | solution.py:77
  232.0 1.3 copy.54
  233.3 14.1 %gather_fusion.2 = f32[4096,32]{1,0:T(8,128)} fusion(f32[32,2048]{0,1:T(8,128)S(1)} %copy.54, s32[4096]{0:T(1024)S(1)} %bitcast_clamp_fusion), kind=kCustom, calls=%fused_computation.1.clone | custom fusion | bytes 1064960 | tf_op jit(solution)/shard_map/jit(_take)/gather | solution.py:73
  247.4 3.2 fusion.9
  250.6 36.3 %reduce-scatter.6.cloned.1.call-done = f32[32,128]{0,1:T(8,128)} async-done(((f32[32,2048]{0,1:T(8,128)}), f32[32,128]{0,1:T(8,128)}) %reduce-scatter.6.cloned.1.call-update) | async-done | bytes 16400 | tf_op jit(solution)/shard_map/reduce_scatter | solution.py:79
  286.9 0.8 add_multiply_fusion.1
  287.8 22.6 %all_gather.15 = f32[32,2048]{0,1:T(8,128)S(1)} all-gather(f32[32,128]{0,1:T(8,128)S(1)} %add_multiply_fusion.1), channel_id=1, replica_groups=mesh['groups'=2,'rows'=16] {'rows'}, dimensions={1}, use_global_device_ids=true | all-gather | bytes 278528 | tf_op jit(solution)/shard_map/all_gather | solution.py:67
  310.3 1.8 fusion.66
  312.2 2.9 cholesky.70
  315.8 0.7 fusion.41
  316.5 2.4 custom-call.14
  318.9 1.2 fusion.45
  320.2 0.7 copy-done.1
  321.6 23.4 %scatter_custom_fusion.2 = f32[32,2048]{0,1:T(8,128)} fusion(s32[4096]{0:T(1024)S(1)} %bitcast.100, f32[32,4096]{0,1:T(8,128)S(1)} %bitcast_multiply_fusion, f32[]{:T(128)} %constant.102.clone.1), kind=kCustom, calls=%fused_computation.12 | custom fusion | flops 131072 | bytes 2359300 | tf_op jit(solution)/shard_map/scatter-add | solution.py:77
  345.0 1.3 copy.57
  346.3 14.1 %gather_fusion.3 = f32[4096,32]{1,0:T(8,128)} fusion(f32[32,2048]{0,1:T(8,128)S(1)} %copy.57, s32[4096]{0:T(1024)S(1)} %bitcast_clamp_fusion), kind=kCustom, calls=%fused_computation.2.clone | custom fusion | bytes 1064960 | tf_op jit(solution)/shard_map/jit(_take)/gather | solution.py:73
  360.4 3.2 fusion.6
  363.6 36.6 %reduce-scatter.8.cloned.1.call-done = f32[32,128]{0,1:T(8,128)} async-done(((f32[32,2048]{0,1:T(8,128)}), f32[32,128]{0,1:T(8,128)}) %reduce-scatter.8.cloned.1.call-update) | async-done | bytes 16400 | tf_op jit(solution)/shard_map/reduce_scatter | solution.py:79
  400.2 1.2 fusion.39
  401.3 57.6 %psum.7 = f32[32,32]{0,1:T(8,128)S(1)} all-reduce(f32[32,32]{0,1:T(8,128)S(1)} %fusion.39), channel_id=1, replica_groups=mesh['groups'=2,'rows'=16] {'rows'}, use_global_device_ids=true, to_apply=%region_12.16 | all-reduce | flops 1024 | bytes 8192 | tf_op jit(solution)/shard_map/psum | solution.py:82
  459.0 2.9 cholesky.81
  462.0 0.6 compare_reduce_fusion
  462.6 0.7 fusion.42
  463.3 2.4 custom-call.9
  465.7 1.7 fusion.38
  (51 shorter events, 4.3 us)
Async XLA Ops:
  7.2 4.3 copy-start
  7.2 51.1 %all-gather.2.cloned.1.call-start = ((), (), s32[]{:S(2)}) async-start(), calls=%async_computation.3 | async-start | bytes 1114112 | tf_op jit(solution)/shard_map/all_gather | solution.py:44
  8.2 3.2 collective-permute-start
  11.5 3.7 copy-start.5
  11.5 3.9 copy-start.6
  15.1 158.6 %reduce-scatter.4.cloned.1.call-start = ((), (), s32[]{:S(2)}) async-start(), calls=%async_computation.4 | async-start | bytes 1114112 | tf_op jit(solution)/shard_map/reduce_scatter | solution.py:79
  41.0 17.3 %copy-start.4 = (bf16[128,256]{1,0:T(8,128)(2,1)S(1)}, bf16[128,256]{1,0:T(8,128)(2,1)}, u32[]{:S(2)}) copy-start(bf16[128,256]{1,0:T(8,128)(2,1)} %multiply_convert_fusion) | copy-start | bytes 196612
  93.0 267.4 %copy-start.3 = (f32[32,128]{1,0:T(8,128)}, f32[32,128]{1,0:T(8,128)S(1)}, u32[]{:S(2)}) copy-start(f32[32,128]{1,0:T(8,128)S(1)} %copy.61) | copy-start | bytes 49156
  117.0 169.9 %reduce-scatter.6.cloned.1.call-start = ((), (), s32[]{:S(2)}) async-start(), calls=%async_computation.5 | async-start | bytes 1114112 | tf_op jit(solution)/shard_map/reduce_scatter | solution.py:79
  206.9 0.7 copy-start.2
  231.8 168.4 %reduce-scatter.8.cloned.1.call-start = ((), (), s32[]{:S(2)}) async-start(), calls=%async_computation.6 | async-start | bytes 1114112 | tf_op jit(solution)/shard_map/reduce_scatter | solution.py:79
  320.2 0.7 copy-start.1
Sparse Core Ops, SparseCore 0:
  15.2 43.0 all-gather.1
  117.1 56.5 reduce-scatter.3
  231.9 54.9 reduce-scatter.5
  345.1 55.0 reduce-scatter.7
where the time goes:
time: 475 us; the launch traced here: 474 us
  waiting for transfers between devices  131 us (28%)
  blocking collectives  128 us (27%)
  other arithmetic  105 us (22%)
  local copies, waits for them, and re-layouts  81.2 us (17%)
  between operations  14 us (3%)
  matrix products  13.5 us (3%)
    reduce_scatter x3, waiting for transfers between devices, on_device(): lax.psum_scatter(spread, 'rows', scatter_dimension=1, tiled=True)  126 us
    all_gather x3, blocking collectives, on_device(): gathered = lax.all_gather(carried, 'rows', axis=1, tiled=True)  70.3 us
    scatter-add x3, other arithmetic, on_device(): spread = jnp.zeros((vec_count, gathered.shape[1]), jnp.float32).at[:, nei...  70.2 us
    psum x1, blocking collectives, on_device(): gram_matrix = lax.psum(partial_gram, 'rows')  57.6 us
    gather x3, local copies, waits for them, and re-layouts, on_device(): jnp.take(gathered, neighbours, axis=1)  42.3 us
    gather x3, local copies, waits for them, and re-layouts, one_block(): jnp.take_along_axis(scores, jnp.clip(relative, 0, block_cols - 1).T, axis=1)  32.9 us
    another operation x9, other arithmetic, on_device(): cholesky_factor = jnp.linalg.cholesky(gram_matrix)  10.8 us
    reduce_sum x3, other arithmetic, on_device(): jnp.sum(affinity[None] * jnp.take(gathered, neighbours, axis=1), axis=1)  9.57 us
  transfers between devices with their start and end apart: 5, of which 5 were waited for; matrix products, arithmetic and copies ran while one was open for 12% of the time, Pallas kernels for 0%

commit v1 on v0

--- a/solution.py
+++ b/solution.py
@@ -79,7 +79,8 @@
         mixed = 0.5 * (forward + lax.psum_scatter(spread, "rows", scatter_dimension=1, tiled=True))
         carried = mixed
     partial_gram = jnp.dot(carried, carried.T, precision=lax.Precision.HIGHEST)
-    gram_matrix = lax.psum(partial_gram, "rows")
+    obtain_rates = lambda sheet, mesh_dim: jax.lax.all_gather(sheet, axis_name=mesh_dim).sum(axis=0)
+    gram_matrix = obtain_rates(partial_gram, "rows")
     cholesky_factor = jnp.linalg.cholesky(gram_matrix)
     carried = jax.scipy.linalg.solve_triangular(cholesky_factor, carried, lower=True)
     return (affinity, carried)

time: 475 us -> 437 us (0.920)
  blocking collectives: 128 us -> 90.4 us
    psum x1 -> x0, blocking collectives: 57.6 us -> none  [on_device(): gram_matrix = lax.psum(partial_gram, 'rows')]
    all_gather x0 -> x1, blocking collectives: none -> 20.1 us  [on_device(): jax.lax.all_gather(sheet, axis_name=mesh_dim).sum(axis=0)]
  transfers between devices with their start and end apart: 5 -> 5, of which waited for: 5 -> 5; matrix products, arithmetic and copies ran while one was open for 12% -> 13% of each run, Pallas kernels for 0% -> 0%
where the time goes in v1:
time: 437 us
  waiting for transfers between devices  131 us (30%)
  other arithmetic  105 us (24%)
  blocking collectives  90.4 us (21%)
  local copies, waits for them, and re-layouts  81.2 us (19%)
  between operations  14 us (3%)
  matrix products  13.5 us (3%)
    reduce_scatter x3, waiting for transfers between devices, on_device(): lax.psum_scatter(spread, 'rows', scatter_dimension=1, tiled=True)  126 us
    all_gather x3, blocking collectives, on_device(): gathered = lax.all_gather(carried, 'rows', axis=1, tiled=True)  70.3 us
    scatter-add x3, other arithmetic, on_device(): spread = jnp.zeros((vec_count, gathered.shape[1]), jnp.float32).at[:, nei...  70.2 us
    gather x3, local copies, waits for them, and re-layouts, on_device(): jnp.take(gathered, neighbours, axis=1)  42.3 us
    gather x3, local copies, waits for them, and re-layouts, one_block(): jnp.take_along_axis(scores, jnp.clip(relative, 0, block_cols - 1).T, axis=1)  32.9 us
    all_gather x1, blocking collectives, on_device(): jax.lax.all_gather(sheet, axis_name=mesh_dim).sum(axis=0)  20.1 us
    another operation x9, other arithmetic, on_device(): cholesky_factor = jnp.linalg.cholesky(gram_matrix)  10.8 us
    reduce_sum x3, other arithmetic, on_device(): jnp.sum(affinity[None] * jnp.take(gathered, neighbours, axis=1), axis=1)  9.57 us
  transfers between devices with their start and end apart: 5, of which 5 were waited for; matrix products, arithmetic and copies ran while one was open for 13% of the time, Pallas kernels for 0%

profile of v1, /device:TPU:0, one launch (start us, length us, event | category | flops | bytes accessed | tf_op | source)
XLA Modules:
  0.0 436.5 jit_solution(13941462872940119483)
XLA Ops:
  7.2 1.0 slice.17
  8.2 1.3 collective-permute-start
  9.5 0.7 broadcast_add_fusion
  10.2 1.3 collective-permute-done
  11.5 2.9 multiply_reduce_fusion
  14.3 0.7 multiply_convert_fusion
  15.4 25.2 %all_gather.19 = f32[32,2048]{1,0:T(8,128)S(1)} all-gather(f32[32,128]{1,0:T(8,128)S(1)} %convert_multiply_fusion), channel_id=1, replica_groups=mesh['groups'=2,'rows'=16] {'rows'}, dimensions={1}, use_global_device_ids=true | all-gather | bytes 278528 | tf_op jit(solution)/shard_map/all_gather | solution.py:67
  41.1 14.1 %gather_fusion.1 = f32[4096,32]{1,0:T(8,128)} fusion(f32[32,2048]{0,1:T(8,128)S(1)} %copy.61, s32[4096]{0:T(1024)S(1)} %bitcast_clamp_fusion), kind=kCustom, calls=%fused_computation.clone | custom fusion | bytes 1064960 | tf_op jit(solution)/shard_map/jit(_take)/gather | solution.py:73
  55.2 3.1 all-gather.3.cloned.1.call-done
  58.3 1.7 fusion.64
  60.0 32.8 %gather_fusion = f32[4096]{0:T(1024)S(1)} fusion(f32[128,2048]{1,0:T(8,128)S(1)} %fusion.64, s32[4096]{0:T(1024)S(1)} %reshape.113), kind=kCustom, calls=%fused_computation.3 | custom fusion | bytes 65536 | tf_op jit(solution)/shard_map/while/body/eval_jaxpr/jit(take_along_axis)/gather | solution.py:56
  93.6 23.4 %scatter_custom_fusion = f32[32,2048]{0,1:T(8,128)} fusion(s32[4096]{0:T(1024)S(1)} %bitcast.100, f32[32,4096]{0,1:T(8,128)S(1)} %bitcast_multiply_fusion.4, f32[]{:T(128)} %constant.102.clone.1), kind=kCustom, calls=%fused_computation.22 | custom fusion | flops 131072 | bytes 2359300 | tf_op jit(solution)/shard_map/scatter-add | solution.py:77
  117.1 3.2 fusion.12
  120.3 53.4 %reduce-scatter.4.cloned.1.call-done = f32[32,128]{0,1:T(8,128)} async-done(((f32[32,2048]{0,1:T(8,128)}), f32[32,128]{0,1:T(8,128)}) %reduce-scatter.4.cloned.1.call-update) | async-done | bytes 16400 | tf_op jit(solution)/shard_map/reduce_scatter | solution.py:79
  173.7 0.8 add_multiply_fusion.2
  174.6 22.6 %all_gather.20 = f32[32,2048]{0,1:T(8,128)S(1)} all-gather(f32[32,128]{0,1:T(8,128)S(1)} %add_multiply_fusion.2), channel_id=1, replica_groups=mesh['groups'=2,'rows'=16] {'rows'}, dimensions={1}, use_global_device_ids=true | all-gather | bytes 278528 | tf_op jit(solution)/shard_map/all_gather | solution.py:67
  197.1 1.8 fusion.65
  199.0 2.9 cholesky.59
  202.0 0.6 compare_reduce_fusion.2
  202.6 0.7 fusion.40
  203.3 2.4 custom-call.13
  205.7 1.2 fusion.48
  207.0 0.7 copy-done.1
  208.4 23.4 %scatter_custom_fusion.1 = f32[32,2048]{0,1:T(8,128)} fusion(s32[4096]{0:T(1024)S(1)} %bitcast.101, f32[32,4096]{0,1:T(8,128)S(1)} %bitcast_multiply_fusion.2, f32[]{:T(128)} %constant.102.clone.1), kind=kCustom, calls=%fused_computation.17 | custom fusion | flops 131072 | bytes 2359300 | tf_op jit(solution)/shard_map/scatter-add | solution.py:77
  232.0 1.3 copy.65
  233.3 14.1 %gather_fusion.2 = f32[4096,32]{1,0:T(8,128)} fusion(f32[32,2048]{0,1:T(8,128)S(1)} %copy.65, s32[4096]{0:T(1024)S(1)} %bitcast_clamp_fusion), kind=kCustom, calls=%fused_computation.1.clone | custom fusion | bytes 1064960 | tf_op jit(solution)/shard_map/jit(_take)/gather | solution.py:73
  247.4 3.2 fusion.9
  250.6 36.3 %reduce-scatter.6.cloned.1.call-done = f32[32,128]{0,1:T(8,128)} async-done(((f32[32,2048]{0,1:T(8,128)}), f32[32,128]{0,1:T(8,128)}) %reduce-scatter.6.cloned.1.call-update) | async-done | bytes 16400 | tf_op jit(solution)/shard_map/reduce_scatter | solution.py:79
  286.9 0.8 add_multiply_fusion.1
  287.8 22.6 %all_gather.21 = f32[32,2048]{0,1:T(8,128)S(1)} all-gather(f32[32,128]{0,1:T(8,128)S(1)} %add_multiply_fusion.1), channel_id=1, replica_groups=mesh['groups'=2,'rows'=16] {'rows'}, dimensions={1}, use_global_device_ids=true | all-gather | bytes 278528 | tf_op jit(solution)/shard_map/all_gather | solution.py:67
  310.3 1.8 fusion.66
  312.2 2.9 cholesky.70
  315.2 0.6 compare_reduce_fusion.1
  315.8 0.7 fusion.41
  316.5 2.4 custom-call.14
  318.9 1.2 fusion.45
  320.2 0.7 copy-done.2
  321.6 23.4 %scatter_custom_fusion.2 = f32[32,2048]{0,1:T(8,128)} fusion(s32[4096]{0:T(1024)S(1)} %bitcast.102, f32[32,4096]{0,1:T(8,128)S(1)} %bitcast_multiply_fusion, f32[]{:T(128)} %constant.102.clone.1), kind=kCustom, calls=%fused_computation.12 | custom fusion | flops 131072 | bytes 2359300 | tf_op jit(solution)/shard_map/scatter-add | solution.py:77
  345.0 1.3 copy.68
  346.3 14.1 %gather_fusion.3 = f32[4096,32]{1,0:T(8,128)} fusion(f32[32,2048]{0,1:T(8,128)S(1)} %copy.68, s32[4096]{0:T(1024)S(1)} %bitcast_clamp_fusion), kind=kCustom, calls=%fused_computation.2.clone | custom fusion | bytes 1064960 | tf_op jit(solution)/shard_map/jit(_take)/gather | solution.py:73
  360.4 3.2 fusion.6
  363.6 36.6 %reduce-scatter.8.cloned.1.call-done = f32[32,128]{0,1:T(8,128)} async-done(((f32[32,2048]{0,1:T(8,128)}), f32[32,128]{0,1:T(8,128)}) %reduce-scatter.8.cloned.1.call-update) | async-done | bytes 16400 | tf_op jit(solution)/shard_map/reduce_scatter | solution.py:79
  400.2 1.2 fusion.39
  401.3 20.1 %all-gather = f32[512,32]{1,0:T(8,128)S(1)} all-gather(f32[32,32]{1,0:T(8,128)S(1)} %fusion.39), channel_id=2, replica_groups=mesh['groups'=2,'rows'=16] {'rows'}, dimensions={0}, use_global_device_ids=true | all-gather | bytes 69632 | tf_op jit(solution)/shard_map/all_gather | solution.py:82
  421.6 2.9 cholesky.81
  425.2 0.7 fusion.42
  425.8 2.4 custom-call.9
  428.3 1.7 fusion.38
  (52 shorter events, 4.4 us)
Async XLA Ops:
  7.2 4.3 copy-start
  7.2 51.1 %all-gather.3.cloned.1.call-start = ((), (), s32[]{:S(2)}) async-start(), calls=%async_computation.3 | async-start | bytes 1114112 | tf_op jit(solution)/shard_map/all_gather | solution.py:44
  8.2 3.2 collective-permute-start
  11.5 3.7 copy-start.5
  11.5 3.9 copy-start.6
  15.1 158.6 %reduce-scatter.4.cloned.1.call-start = ((), (), s32[]{:S(2)}) async-start(), calls=%async_computation.4 | async-start | bytes 1114112 | tf_op jit(solution)/shard_map/reduce_scatter | solution.py:79
  41.0 17.3 %copy-start.4 = (bf16[128,256]{1,0:T(8,128)(2,1)S(1)}, bf16[128,256]{1,0:T(8,128)(2,1)}, u32[]{:S(2)}) copy-start(bf16[128,256]{1,0:T(8,128)(2,1)} %multiply_convert_fusion) | copy-start | bytes 196612
  93.0 267.4 %copy-start.3 = (f32[32,128]{1,0:T(8,128)}, f32[32,128]{1,0:T(8,128)S(1)}, u32[]{:S(2)}) copy-start(f32[32,128]{1,0:T(8,128)S(1)} %copy.71) | copy-start | bytes 49156
  117.0 169.9 %reduce-scatter.6.cloned.1.call-start = ((), (), s32[]{:S(2)}) async-start(), calls=%async_computation.5 | async-start | bytes 1114112 | tf_op jit(solution)/shard_map/reduce_scatter | solution.py:79
  206.9 0.7 copy-start.1
  231.8 168.4 %reduce-scatter.8.cloned.1.call-start = ((), (), s32[]{:S(2)}) async-start(), calls=%async_computation.6 | async-start | bytes 1114112 | tf_op jit(solution)/shard_map/reduce_scatter | solution.py:79
  320.2 0.7 copy-start.2
Sparse Core Ops, SparseCore 0:
  15.2 43.0 all-gather.2
  117.1 56.5 reduce-scatter.3
  231.9 54.9 reduce-scatter.5
  345.1 55.0 reduce-scatter.7
